TPU v7x, 128 devices: a whole 4x4x4 slice. The times are simulated.
128 devices in a mesh: freq: 64 (over z, y, x_hi, core), kpt: 2 (over x_lo).
Axes of the slice: x: 4 (x_hi: 2, x_lo: 2; x = x_hi * 2 + x_lo), y: 4, z: 4, core: 2. Of those that a mesh axis runs over, the one named last changes fastest.
Arguments:
- band_energy: float32 [2, 384], P('kpt'), may hold values from -4.5 to 4.5, as said below
- projector: bfloat16 [2, 640, 384], P('kpt', 'freq'), may hold values from -0.25 to 0.25
- sigma: float32 [2, 5, 5, 128, 64], P(None, None, None, 'freq'), may hold values from -8.5 to 8.5, as said below
- atom_of_slot: int32 [128], replicated, may hold values from 0 to 127, each once
- kweight: int32 [2], replicated, may hold values from 1 to 16
Outputs:
- local_green: float32 [2, 5, 5, 128, 64], P(None, None, None, ('freq', 'kpt'))
Inputs may be any that keep to these rules, and one draw needn't show every extreme that they name: `band_energy`: every entry is a band energy; the energies of one k-point share a common offset drawn per k-point. Each block sigma[0, :, :, s, n] is symmetric; each block sigma[1, :, :, s, n] is symmetric and negative definite. `atom_of_slot`: A permutation of 0 to 127; slot s belongs to the owner s // (128 // 64) along freq.
All inputs are finite; a program needn't handle non-finite values.
Results may differ from a plain program's by a relative error of at most 0.0003.
Values may be sent and summed in bfloat16 or wider, within the bound.
No kernel may reach another device: no remote copies, remote signals or barrier semaphores. Data moves between devices by JAX's collectives and lax.ppermute only.
A program may use at most 64 MiB of HBM per device.

v0:
```python
import math

import jax
import jax.numpy as jnp
from jax import lax
from jax.sharding import PartitionSpec as P

BANDS = 384
ATOMS = 128
ORBS = 5


HIGH = lax.Precision.HIGHEST
BETA_INV = 0.1


def copy_for_each(array, axis):
    copies = jnp.broadcast_to(array, (lax.axis_size(axis), *array.shape))
    return lax.all_to_all(copies, axis, split_axis=0, concat_axis=0, tiled=True)


def in_order(parts, dim):
    shape = list(parts.shape[1:])
    shape[dim] *= parts.shape[0]
    return jnp.moveaxis(parts, 0, dim).reshape(shape)


def collect(array, axis, dim):
    parts = copy_for_each(array, axis)
    return in_order(parts, dim)


def split_up(array, dim, count):
    before, after = (array.shape[:dim], array.shape[dim + 1 :])
    return jnp.moveaxis(array.reshape(*before, count, -1, *after), dim, 0)


def sum_at_owner(array, axis, dim):
    parts = split_up(array, dim, lax.axis_size(axis))
    arrived = lax.all_to_all(parts, axis, split_axis=0, concat_axis=0, tiled=True)
    return arrived.sum(axis=0)


def local_block(energy, proj, real_sig, imag_sig, omega):
    proj3 = proj.reshape(ATOMS, ORBS, BANDS).astype(jnp.float32)
    real_rows = (
        jnp.einsum("amo,aob->amb", real_sig, proj3, precision=HIGH)
        .reshape(ATOMS * ORBS, BANDS)
        .astype(jnp.bfloat16)
    )
    imag_rows = (
        jnp.einsum("amo,aob->amb", imag_sig, proj3, precision=HIGH)
        .reshape(ATOMS * ORBS, BANDS)
        .astype(jnp.bfloat16)
    )
    up_real = jnp.dot(proj.T, real_rows, preferred_element_type=jnp.float32)
    up_imag = jnp.dot(proj.T, imag_rows, preferred_element_type=jnp.float32)
    eye = jnp.eye(BANDS, dtype=jnp.float32)
    x_mat = -jnp.diag(energy) - 0.5 * (up_real + up_real.T)
    y_mat = omega * eye - 0.5 * (up_imag + up_imag.T)
    lower = jnp.linalg.cholesky(y_mat)
    left = jax.scipy.linalg.solve_triangular(lower, x_mat, lower=True)
    core = jax.scipy.linalg.solve_triangular(lower, left.T, lower=True)
    core = 0.5 * (core + core.T)
    square = jnp.dot(core, core, precision=HIGH) + eye
    factor = jnp.linalg.cholesky(square)
    upper_rows = jax.scipy.linalg.solve_triangular(lower, proj.astype(jnp.float32).T, lower=True).T
    solved = jax.scipy.linalg.cho_solve((factor, True), upper_rows.T)
    wide = solved.T.reshape(ATOMS, ORBS, BANDS)
    turned = jnp.dot(upper_rows, core, precision=HIGH).reshape(ATOMS, ORBS, BANDS)
    real_part = jnp.einsum("amb,aob->amo", turned, wide, precision=HIGH)
    imag_part = -jnp.einsum(
        "amb,aob->amo", upper_rows.reshape(ATOMS, ORBS, BANDS), wide, precision=HIGH
    )
    return jnp.stack([real_part, imag_part])


def local(band_energy, projector, sigma, atom_of_slot, kweight):
    freq_count = lax.axis_size("freq")
    freq_index = lax.axis_index("freq")
    kpt_index = lax.axis_index("kpt")
    points = band_energy.shape[0]
    all_freqs = sigma.shape[4]
    per_freq = all_freqs // freq_count
    projections = collect(projector, "freq", 1)
    sig_here = lax.all_to_all(sigma, "freq", split_axis=4, concat_axis=3, tiled=True)
    onehot = (atom_of_slot[:, None] == jnp.arange(ATOMS, dtype=jnp.int32)[None, :]).astype(
        jnp.float32
    )
    sig_atom = jnp.einsum("xmosf,sa->xmoaf", sig_here, onehot, precision=HIGH)
    weights = kweight.astype(jnp.float32)
    total = jnp.sum(weights)
    own_weights = lax.dynamic_slice_in_dim(weights, kpt_index * points, points, 0)
    number = freq_index * per_freq + 0
    omega = (2.0 * number.astype(jnp.float32) + 1.0) * math.pi * BETA_INV
    real_sig = jnp.transpose(sig_atom[0, :, :, :, 0], (2, 0, 1))
    imag_sig = jnp.transpose(sig_atom[1, :, :, :, 0], (2, 0, 1))

    def add_point(point, acc):
        energy = lax.dynamic_index_in_dim(band_energy, point, 0, keepdims=False)
        proj = lax.dynamic_index_in_dim(projections, point, 0, keepdims=False)
        block = local_block(energy, proj, real_sig, imag_sig, omega)
        return acc + own_weights[point] * block

    summed = lax.fori_loop(0, points, add_point, jnp.zeros((2, ATOMS, ORBS, ORBS), jnp.float32))
    columns = [jnp.einsum("xamo,sa->xmos", summed, onehot, precision=HIGH)]
    partial_blocks = jnp.stack(columns, axis=4)
    owned = lax.all_to_all(partial_blocks, "freq", split_axis=3, concat_axis=4, tiled=True)
    result = sum_at_owner(owned, "kpt", 3)
    return result / total


def solution(mesh):
    placed = (P("kpt", None), P("kpt", "freq", None), P(None, None, None, "freq", None), P(), P())
    return jax.shard_map(
        local,
        mesh=mesh,
        in_specs=placed,
        out_specs=P(None, None, None, ("freq", "kpt"), None),
        check_vma=False,
    )
```

profile of v0, /device:TPU:1, one launch (start us, length us, event | category | flops | bytes accessed | tf_op | source)
XLA Modules:
  0.0 329.4 jit_solution(4363684923110968006)
XLA Ops:
  1.3 27.9 %all_to_all.40 = f32[2,5,5,2,64]{2,3,1,0,4:T(2,128)S(1)} all-to-all(f32[2,5,5,2,64]{2,3,1,0,4:T(2,128)S(1)} %copy.148), channel_id=1, replica_groups=mesh['freq'=64,'kpt'=2] {'freq'}, dimensions={4} | all-to-all | bytes 51200 | tf_op jit(solution)/shard_map/all_to_all | solution.py:86
  30.1 5.2 %all-to-all-start.1 = ((bf16[64,1,10,384]{3,2,1,0:T(8,128)(2,1)}), bf16[64,1,10,384]{3,2,1,0:T(8,128)(2,1)S(1)}, u32[]{:S(2)}, u32[]{:S(2)}) async-start(bf16[64,1,10,384]{3,2,1,0:T(8,128)(2,1)} %broadcast_in_dim.30), calls=%async_computation.1 | async-start | bytes 1572864 | tf_op jit(solution)/shard_map/all_to_all | solution.py:19
  38.3 13.7 %all-to-all-done.1 = bf16[64,1,10,384]{3,2,1,0:T(8,128)(2,1)S(1)} async-done(((bf16[64,1,10,384]{3,2,1,0:T(8,128)(2,1)}), bf16[64,1,10,384]{3,2,1,0:T(8,128)(2,1)S(1)}, u32[]{:S(2)}, u32[]{:S(2)}) %all-to-all-start.1) | async-done | bytes 491552 | tf_op jit(solution)/shard_map/all_to_all | solution.py:19
  55.7 11.7 %cholesky.208 = f32[128,128]{1,0:T(8,128)S(1)} custom-call(f32[128,128]{1,0:T(8,128)S(1)} %cholesky.310), custom_call_target="Cholesky" | custom-call | tf_op jit(solution)/shard_map/while/body/eval_jaxpr/jit(cholesky)/cholesky | solution.py:61
  67.4 9.8 %custom-call.30 = f32[1,128,128]{1,2,0:T(8,128)S(1)} custom-call(f32[1,128,128]{2,1,0:T(8,128)S(1)} %get-tuple-element.153), custom_call_target="InvertDiagBlocksLowerTriangular" | custom-call | tf_op jit(solution)/shard_map/while/body/eval_jaxpr/jit(cholesky)/cholesky | solution.py:61
  77.9 11.9 %cholesky.227 = f32[128,128]{1,0:T(8,128)S(1)} custom-call(f32[128,128]{1,0:T(8,128)S(1)} %cholesky.314), custom_call_target="Cholesky" | custom-call | tf_op jit(solution)/shard_map/while/body/eval_jaxpr/jit(cholesky)/cholesky | solution.py:61
  89.8 9.8 %custom-call.31 = f32[1,128,128]{1,2,0:T(8,128)S(1)} custom-call(f32[1,128,128]{2,1,0:T(8,128)S(1)} %get-tuple-element.150), custom_call_target="InvertDiagBlocksLowerTriangular" | custom-call | tf_op jit(solution)/shard_map/while/body/eval_jaxpr/jit(cholesky)/cholesky | solution.py:61
  100.9 11.7 %cholesky.246 = f32[128,128]{1,0:T(8,128)S(1)} custom-call(f32[128,128]{1,0:T(8,128)S(1)} %convolution_subtract_fusion.13), custom_call_target="Cholesky" | custom-call | tf_op jit(solution)/shard_map/while/body/eval_jaxpr/jit(cholesky)/cholesky | solution.py:61
  116.0 6.1 %while.15 = (s32[]{:T(128)}, f32[384,384]{1,0:T(8,128)S(1)}, s32[3,2]{0,1:T(2,128)S(1)}, f32[3,128,128]{2,1,0:T(8,128)S(1)}, s32[]{:T(128)}) while((s32[]{:T(128)}, f32[384,384]{1,0:T(8,128)S(1)}, s32[3,2]{0,1:T(2,128)S(1)}, f32[3,128,128]{2,1,0:T(8,128)S(1)}, s32[]{:T(128)}) %tuple.70), condition=%wide.while_cond, body=%wide.while_body.sunk | while | flops 2 | bytes 131181 | solution.py:67
  122.1 29.7 %custom-call.32 = f32[3,128,128]{1,2,0:T(8,128)S(1)} custom-call(f32[3,128,128]{2,1,0:T(8,128)S(1)} %get-tuple-element.71), custom_call_target="InvertDiagBlocksLowerTriangular" | custom-call | tf_op jit(solution)/shard_map/while/body/eval_jaxpr/jit(_solve_triangular)/triangular_solve/custom-call.0 | solution.py:67
  161.6 11.7 %cholesky.261 = f32[128,128]{1,0:T(8,128)S(1)} custom-call(f32[128,128]{1,0:T(8,128)S(1)} %cholesky.318), custom_call_target="Cholesky" | custom-call | tf_op jit(solution)/shard_map/while/body/eval_jaxpr/jit(cholesky)/cholesky | solution.py:66
  173.4 10.2 %custom-call.35 = f32[1,128,128]{1,2,0:T(8,128)S(1)} custom-call(f32[1,128,128]{2,1,0:T(8,128)S(1)} %get-tuple-element.146), custom_call_target="InvertDiagBlocksLowerTriangular" | custom-call | tf_op jit(solution)/shard_map/while/body/eval_jaxpr/jit(cholesky)/cholesky | solution.py:66
  186.0 11.7 %cholesky.280 = f32[128,128]{1,0:T(8,128)S(1)} custom-call(f32[128,128]{1,0:T(8,128)S(1)} %cholesky.322), custom_call_target="Cholesky" | custom-call | tf_op jit(solution)/shard_map/while/body/eval_jaxpr/jit(cholesky)/cholesky | solution.py:66
  198.0 9.8 %custom-call.36 = f32[1,128,128]{1,2,0:T(8,128)S(1)} custom-call(f32[1,128,128]{2,1,0:T(8,128)S(1)} %get-tuple-element.144), custom_call_target="InvertDiagBlocksLowerTriangular" | custom-call | tf_op jit(solution)/shard_map/while/body/eval_jaxpr/jit(cholesky)/cholesky | solution.py:66
  210.3 11.9 %cholesky.299 = f32[128,128]{1,0:T(8,128)S(1)} custom-call(f32[128,128]{1,0:T(8,128)S(1)} %convolution_subtract_fusion.12), custom_call_target="Cholesky" | custom-call | tf_op jit(solution)/shard_map/while/body/eval_jaxpr/jit(cholesky)/cholesky | solution.py:66
  226.0 3.2 fusion.1
  237.6 6.6 %while.14 = (s32[]{:T(128)}, f32[384,384]{0,1:T(8,128)S(1)}, s32[3,2]{0,1:T(2,128)S(1)}, f32[3,128,128]{2,1,0:T(8,128)S(1)}, s32[]{:T(128)}) while((s32[]{:T(128)}, f32[384,384]{0,1:T(8,128)S(1)}, s32[3,2]{0,1:T(2,128)S(1)}, f32[3,128,128]{2,1,0:T(8,128)S(1)}, s32[]{:T(128)}) %tuple.76), condition=%wide.while_cond.2, body=%wide.while_body.2.sunk | while | flops 2 | bytes 393321 | solution.py:68
  244.9 30.5 %custom-call.25 = f32[3,128,128]{1,2,0:T(8,128)S(1)} custom-call(f32[3,128,128]{2,1,0:T(8,128)} %copy-done.7), custom_call_target="InvertDiagBlocksLowerTriangular" | custom-call | tf_op jit(solution)/shard_map/while/body/eval_jaxpr/jit(_cho_solve)/triangular_solve | solution.py:68
  282.9 4.6 %convolution_bitcast_fusion = f32[1,128,5,5]{3,2,1,0:T(8,128)} fusion(f32[128,5,384]{2,1,0:T(8,128)S(1)} %reshape.94, f32[128,5,384]{2,1,0:T(8,128)S(1)} %reshape.95), kind=kOutput, calls=%fused_computation.7 | convolution fusion | flops 14745600 | bytes 1978880 | tf_op jit(solution)/shard_map/while/body/eval_jaxpr/amb,aob->amo/dot_general | solution.py:71
  288.6 2.5 copy.173
  292.5 4.6 %fusion.86 = f32[128,5,5]{2,1,0:T(8,128)} fusion(f32[128,5,384]{2,1,0:T(8,128)S(1)} %reshape.96, f32[128,5,384]{2,1,0:T(8,128)S(1)} %reshape.95), kind=kOutput, calls=%fused_computation.161 | convolution fusion | flops 14745600 | bytes 1978880 | tf_op jit(solution)/shard_map/while/body/eval_jaxpr/amb,aob->amo/dot_general | solution.py:72
  299.6 19.8 %all_to_all.41 = f32[2,5,5,128,1]{2,0,4,1,3:T(2,128)S(1)} all-to-all(f32[2,5,5,128,1]{2,0,4,1,3:T(2,128)S(1)} %copy.176), channel_id=1, replica_groups=mesh['freq'=64,'kpt'=2] {'freq'}, dimensions={3} | all-to-all | bytes 51200 | tf_op jit(solution)/shard_map/all_to_all | solution.py:108
  320.5 3.2 all-to-all-start.3
  324.4 2.1 all-to-all-done.3
  (168 shorter events, 67.2 us)
Async XLA Ops:
  0.0 29.2 %copy-start.8 = (bf16[1,10,384]{2,1,0:T(8,128)(2,1)S(1)}, bf16[1,10,384]{2,1,0:T(8,128)(2,1)}, u32[]{:S(2)}) copy-start(bf16[1,10,384]{2,1,0:T(8,128)(2,1)} %param.11) | copy-start | bytes 23044
  1.2 34.1 %copy-start.11 = (s32[2]{0:T(128)S(1)}, s32[2]{0:T(128)}, u32[]{:S(2)}) copy-start(s32[2]{0:T(128)} %param.14) | copy-start | bytes 28
  1.3 34.1 %copy-start.10 = (f32[1,384]{1,0:T(1,128)S(1)}, f32[1,384]{1,0:T(1,128)}, u32[]{:S(2)}) copy-start(f32[1,384]{1,0:T(1,128)} %param.10) | copy-start | bytes 4612
  30.1 6.2 %copy-start.9 = (s32[128]{0:T(128)S(1)}, s32[128]{0:T(128)}, u32[]{:S(2)}) copy-start(s32[128]{0:T(128)} %param.13) | copy-start | bytes 1540
  30.1 21.8 %all-to-all-start.1 = ((bf16[64,1,10,384]{3,2,1,0:T(8,128)(2,1)}), bf16[64,1,10,384]{3,2,1,0:T(8,128)(2,1)S(1)}, u32[]{:S(2)}, u32[]{:S(2)}) async-start(bf16[64,1,10,384]{3,2,1,0:T(8,128)(2,1)} %broadcast_in_dim.30), calls=%async_computation.1 | async-start | bytes 1572864 | tf_op jit(solution)/shard_map/all_to_all | solution.py:19
  55.6 21.9 %copy-start.6 = (f32[384,384]{1,0:T(8,128)}, f32[384,384]{1,0:T(8,128)S(1)}, u32[]{:S(2)}) copy-start(f32[384,384]{1,0:T(8,128)S(1)} %fusion.15) | copy-start | bytes 1769476
  77.8 74.0 %copy-start.3 = (f32[128,5,5]{2,1,0:T(8,128)S(1)}, f32[128,5,5]{2,1,0:T(8,128)}, u32[]{:S(2)}) copy-start(f32[128,5,5]{2,1,0:T(8,128)} %copy.155) | copy-start | bytes 38404
  158.9 1.6 copy-start
  160.8 0.8 copy-start.5
  183.6 39.9 %copy-start.4 = (bf16[640,384]{0,1:T(8,128)(2,1)S(1)}, bf16[640,384]{0,1:T(8,128)(2,1)}, u32[]{:S(2)}) copy-start(bf16[640,384]{0,1:T(8,128)(2,1)} %copy.154) | copy-start | bytes 1474564
  208.2 0.8 copy-start.2
  224.5 1.5 copy-start.1
  244.2 0.7 copy-start.7
  299.6 24.1 %copy-start.12 = (s32[2]{0:T(128)S(1)}, s32[2]{0:T(128)}, u32[]{:S(2)}) copy-start(s32[2]{0:T(128)} %param.14) | copy-start | bytes 28
  320.5 6.0 %all-to-all-start.3 = ((f32[2,1,3200]{2,1,0:T(1,128)}), f32[2,1,3200]{2,1,0:T(1,128)S(1)}, u32[]{:S(2)}, u32[]{:S(2)}) async-start(f32[2,1,3200]{2,1,0:T(1,128)} %reshape.172), calls=%async_computation.3 | async-start | bytes 51200 | tf_op jit(solution)/shard_map/all_to_all | solution.py:40
where the time goes:
time: 333 us; the launch traced here: 329 us
  other arithmetic  181 us (54%)
  blocking collectives  47.7 us (14%)
  local copies, waits for them, and re-layouts  36.6 us (11%)
  matrix products  35.2 us (11%)
  waiting for transfers between devices  15.7 us (5%)
  starting transfers between devices  8.45 us (3%)
  between operations  4.84 us (1%)
    another operation x11, other arithmetic, local_block(): factor = jnp.linalg.cholesky(square)  58.6 us
    another operation x10, other arithmetic, local_block(): lower = jnp.linalg.cholesky(y_mat)  56.4 us
    another operation x2, other arithmetic, local_block(): solved = jax.scipy.linalg.cho_solve((factor, True), upper_rows.T)  31.6 us
    another operation x3, other arithmetic, local_block(): jax.scipy.linalg.solve_triangular(lower, proj.astype(jnp.float32).T, lowe...  29.8 us
    all_to_all x1, blocking collectives, local(): lax.all_to_all(sigma, 'freq', split_axis=4, concat_axis=3, tiled=True)  27.9 us
    all_to_all x1, blocking collectives, local(): lax.all_to_all(partial_blocks, 'freq', split_axis=3, concat_axis=4, tiled...  19.8 us
    all_to_all x1, waiting for transfers between devices, copy_for_each(): return lax.all_to_all(copies, axis, split_axis=0, concat_axis=0, tiled=True)  13.7 us
  transfers between devices with their start and end apart: 2, of which 2 were waited for; matrix products, arithmetic and copies ran while one was open for 1% of the time, Pallas kernels for 0%

commit v1 on v0

v1 whole, which is shorter than its diff:
```python
import math

import jax
import jax.numpy as jnp
from jax import lax
from jax.experimental import pallas as pl
from jax.experimental.pallas import tpu as pltpu
from jax.sharding import PartitionSpec as P

BANDS = 384
ATOMS = 128
ORBS = 5
PARTS = 2 * ORBS * ORBS
BETA_INV = 0.1
LANES = 128
CHUNKS = BANDS // LANES
ROWS = 8
PANELS = LANES // ROWS

f32 = jnp.float32
bf16 = jnp.bfloat16


def split3(x):
    hi = x.astype(bf16)
    rest = x - hi.astype(f32)
    mid = rest.astype(bf16)
    low = (rest - mid.astype(f32)).astype(bf16)
    return hi, mid, low


def pack_kernel(proj_ref, sig_ref, out_ref, tmp_ref):
    tmp_ref[...] = jnp.zeros_like(tmp_ref)
    tmp_ref[0:PARTS, 0:64] = sig_ref[:, 0, :]
    tmp_ref[64 : 64 + PARTS, 0:64] = sig_ref[:, 1, :]
    turned = tmp_ref[...].T
    hi, mid, low = split3(turned)
    parts = [hi.astype(f32), mid.astype(f32), low.astype(f32)]
    rows = lax.broadcasted_iota(jnp.int32, (16, LANES), 0)
    base = [
        jnp.concatenate(
            [proj_ref[:, LANES * c : LANES * (c + 1)].astype(f32), jnp.zeros((6, LANES), f32)], axis=0
        )
        for c in range(3)
    ]
    for n in range(64):
        for c in range(3):
            row = jnp.broadcast_to(parts[c][n : n + 1, :], (16, LANES))
            out_ref[n, :, LANES * c : LANES * (c + 1)] = jnp.where(rows == 10, row, base[c]).astype(bf16)


def unpack_kernel(in_ref, out_ref):
    both = in_ref[pl.ds(0, 64, stride=2), :] + in_ref[pl.ds(1, 64, stride=2), :]
    turned = both.T
    for i in range(PARTS):
        out_ref[i, :, :] = turned[i : i + 1, :]


def cmul(ar, ai, br, bi):
    return ar * br - ai * bi, ar * bi + ai * br


def row_of(x, i):
    return jnp.broadcast_to(x[i : i + 1, :], (ROWS, LANES))


def lane_of(x, i):
    return jnp.broadcast_to(x[:, i : i + 1], (ROWS, LANES))


def sweep_panel(j, diag, rest, sub_iota, lane_iota):
    first = ROWS * j
    cols = [(lane_of(diag[0], first + t), lane_of(diag[1], first + t)) for t in range(ROWS)]
    in_block = (lane_iota >= first) & (lane_iota < first + ROWS)
    eye = jnp.where(lane_iota == sub_iota + first, 1.0, 0.0).astype(f32)
    work = [(jnp.where(in_block, eye, diag[0]), jnp.where(in_block, 0.0, diag[1]))] + rest
    for p in range(0, ROWS, 2):
        q = p + 1
        ar, ai = row_of(cols[p][0], p), row_of(cols[p][1], p)
        br, bi = row_of(cols[q][0], p), row_of(cols[q][1], p)
        dr, di = row_of(cols[q][0], q), row_of(cols[q][1], q)
        adr, adi = cmul(ar, ai, dr, di)
        bbr, bbi = cmul(br, bi, br, bi)
        det_r, det_i = adr - bbr, adi - bbi
        inv = 1.0 / (det_r * det_r + det_i * det_i)
        vr, vi = det_r * inv, -(det_i * inv)
        w11 = cmul(dr, di, vr, vi)
        w22 = cmul(ar, ai, vr, vi)
        w12 = cmul(-br, -bi, vr, vi)
        cpr, cpi = cols[p]
        cqr, cqi = cols[q]
        t1, t2 = cmul(cpr, cpi, *w11), cmul(cqr, cqi, *w12)
        t3, t4 = cmul(cpr, cpi, *w12), cmul(cqr, cqi, *w22)
        at_p, at_q = sub_iota == p, sub_iota == q
        fp = [jnp.where(at_p, -w11[z], jnp.where(at_q, -w12[z], t1[z] + t2[z])) for z in range(2)]
        fq = [jnp.where(at_p, -w12[z], jnp.where(at_q, -w22[z], t3[z] + t4[z])) for z in range(2)]
        keep = ~(at_p | at_q)

        def step(x):
            xr, xi = x
            pr, pi = row_of(xr, p), row_of(xi, p)
            qr, qi = row_of(xr, q), row_of(xi, q)
            yr = jnp.where(keep, xr, 0.0) - (fp[0] * pr - fp[1] * pi) - (fq[0] * qr - fq[1] * qi)
            yi = jnp.where(keep, xi, 0.0) - (fp[0] * pi + fp[1] * pr) - (fq[0] * qi + fq[1] * qr)
            return yr, yi

        for t in range(q + 1, ROWS):
            cols[t] = step(cols[t])
        work = [step(x) for x in work]
    head_r, head_i = work[0]
    update = [(jnp.where(in_block, eye - head_r, head_r), jnp.where(in_block, -head_i, head_i))] + work[1:]
    final = [(jnp.where(in_block, -head_r, head_r), jnp.where(in_block, -head_i, head_i))] + work[1:]
    return update, final


def stack_parts(top, bottom, order):
    parts = split3(jnp.concatenate([top, bottom], axis=0))
    return jnp.concatenate([parts[i] for i in order], axis=0)


LEFT = (0, 0, 0, 1, 1, 2)
RIGHT = (0, 1, 2, 0, 1, 0)


def main_kernel(buf_ref, atom_ref, energy_ref, weight_ref, out_ref, re_ref, im_ref, rows_ref, out_tmp):
    freq = lax.axis_index("freq")
    kpt = lax.axis_index("kpt")
    omega = (2.0 * freq.astype(f32) + 1.0) * math.pi * BETA_INV
    total = (weight_ref[0] + weight_ref[1]).astype(f32)
    own = jnp.where(kpt == 0, weight_ref[0], weight_ref[1]).astype(f32)

    atom = atom_ref[...]
    base = (atom >> 1) * 16 + (atom & 1) * 5
    lane_row = lax.broadcasted_iota(jnp.int32, (1, LANES), 1)
    target = jnp.concatenate([base + o for o in range(ORBS)] + [(lane_row >> 1) * 16 + 10], axis=1)
    pick = (lax.broadcasted_iota(jnp.int32, (1024, 768), 0) == target).astype(f32).astype(bf16)
    turned = lax.dot_general(
        buf_ref[...], pick, (((0,), (0,)), ((), ())), preferred_element_type=f32
    )
    proj_t = [turned[:, LANES * o : LANES * (o + 1)] for o in range(ORBS)]
    sig_parts = turned[0:128, 640:768] + turned[128:256, 640:768] + turned[256:384, 640:768]
    odd = (lax.broadcasted_iota(jnp.int32, (64, LANES), 1) & 1) == 1
    sig = jnp.where(odd, sig_parts[64:128, :], sig_parts[0:64, :])

    proj_b = turned[:, 0:640].astype(bf16)
    for x in range(2):
        for m in range(ORBS):
            acc = None
            for o in range(ORBS):
                i = x * 25 + m * 5 + o
                term = sig[i : i + 1, :] * proj_t[o]
                acc = term if acc is None else acc + term
            rows_ref[x * BANDS : (x + 1) * BANDS, LANES * m : LANES * (m + 1)] = acc.astype(bf16)
    ups = lax.dot_general(
        rows_ref[...], proj_b, (((1,), (1,)), ((), ())), preferred_element_type=f32
    )
    up_r, up_i = ups[0:BANDS, :], ups[BANDS : 2 * BANDS, :]
    ii = lax.broadcasted_iota(jnp.int32, (BANDS, BANDS), 0)
    jj = lax.broadcasted_iota(jnp.int32, (BANDS, BANDS), 1)
    x_mat = jnp.where(ii == jj, -energy_ref[...], 0.0) - 0.5 * (up_r + up_r.T)
    y_mat = jnp.where(ii == jj, omega, 0.0) - 0.5 * (up_i + up_i.T)
    for c in range(CHUNKS):
        re_ref[c, :, :] = x_mat[:, LANES * c : LANES * (c + 1)]
        im_ref[c, :, :] = y_mat[:, LANES * c : LANES * (c + 1)]

    sub_iota = lax.broadcasted_iota(jnp.int32, (ROWS, LANES), 0)
    lane_iota = lax.broadcasted_iota(jnp.int32, (ROWS, LANES), 1)

    def block_step(kb, carry):
        chunk = [kb, lax.rem(kb + 1, CHUNKS), lax.rem(kb + 2, CHUNKS)]
        for j in range(PANELS):
            at = pl.ds(pl.multiple_of(kb * LANES + ROWS * j, ROWS), ROWS)
            panel = [(re_ref[c, at, :], im_ref[c, at, :]) for c in chunk]
            update, final = sweep_panel(j, panel[0], panel[1:], sub_iota, lane_iota)
            left = jnp.concatenate(
                [stack_parts(r, i, LEFT) for r, i in panel], axis=1
            )
            for z in range(CHUNKS):
                r, i = update[z]
                right = stack_parts(
                    jnp.concatenate([r, i], axis=1), jnp.concatenate([-i, r], axis=1), RIGHT
                )
                prod = lax.dot_general(left, right, (((0,), (0,)), ((), ())), preferred_element_type=f32)
                for y in range(CHUNKS):
                    here = pl.ds(pl.multiple_of(chunk[y] * LANES, LANES), LANES)
                    piece = prod[LANES * y : LANES * (y + 1), :]
                    re_ref[chunk[z], here, :] = re_ref[chunk[z], here, :] - piece[:, 0:LANES]
                    im_ref[chunk[z], here, :] = im_ref[chunk[z], here, :] - piece[:, LANES:]
            for z in range(CHUNKS):
                re_ref[chunk[z], at, :] = final[z][0]
                im_ref[chunk[z], at, :] = final[z][1]
        return carry

    lax.fori_loop(0, CHUNKS, block_step, 0)

    wide = []
    for ref in (re_ref, im_ref):
        full = jnp.concatenate([ref[c, :, :] for c in range(CHUNKS)], axis=1)
        hi = full.astype(bf16)
        low = (full - hi.astype(f32)).astype(bf16)
        wide.append(jnp.concatenate([hi, low], axis=1))
    left = jnp.concatenate(wide, axis=0)
    twice = jnp.concatenate([proj_b, proj_b], axis=0)
    gp = lax.dot_general(left, twice, (((1,), (0,)), ((), ())), preferred_element_type=f32)
    scale = -own / total
    out_tmp[...] = jnp.zeros_like(out_tmp)
    for x in range(2):
        for m in range(ORBS):
            v = gp[x * BANDS : (x + 1) * BANDS, LANES * m : LANES * (m + 1)]
            for o in range(m, ORBS):
                val = jnp.sum(v * proj_t[o], axis=0, keepdims=True) * scale
                i1, i2 = x * 25 + m * 5 + o, x * 25 + o * 5 + m
                out_tmp[i1 : i1 + 1, :] = val
                if o != m:
                    out_tmp[i2 : i2 + 1, :] = val
    out_ref[...] = out_tmp[...].T


def vmem():
    return pl.BlockSpec(memory_space=pltpu.VMEM)


def local(band_energy, projector, sigma, atom_of_slot, kweight):
    packed = pl.pallas_call(
        pack_kernel,
        out_shape=jax.ShapeDtypeStruct((64, 16, BANDS), bf16),
        in_specs=[vmem(), vmem()],
        out_specs=vmem(),
        scratch_shapes=[pltpu.VMEM((LANES, LANES), f32)],
        name="pack",
    )(projector.reshape(10, BANDS), sigma.reshape(PARTS, 2, 64))
    arrived = lax.all_to_all(packed, "freq", split_axis=0, concat_axis=0, tiled=True)
    blocks = pl.pallas_call(
        main_kernel,
        out_shape=jax.ShapeDtypeStruct((ATOMS, LANES), f32),
        in_specs=[vmem(), vmem(), vmem(), pl.BlockSpec(memory_space=pltpu.SMEM)],
        out_specs=vmem(),
        scratch_shapes=[
            pltpu.VMEM((CHUNKS, BANDS, LANES), f32),
            pltpu.VMEM((CHUNKS, BANDS, LANES), f32),
            pltpu.VMEM((2 * BANDS, 640), bf16),
            pltpu.VMEM((LANES, LANES), f32),
        ],
        name="green",
    )(arrived.reshape(1024, BANDS), atom_of_slot.reshape(1, ATOMS), band_energy, kweight)
    back = lax.all_to_all(
        blocks.reshape(ATOMS, 1, LANES), ("freq", "kpt"), split_axis=0, concat_axis=0, tiled=True
    )
    out = pl.pallas_call(
        unpack_kernel,
        out_shape=jax.ShapeDtypeStruct((PARTS, 1, 64), f32),
        in_specs=[vmem()],
        out_specs=vmem(),
        name="unpack",
    )(back.reshape(ATOMS, LANES))
    return out.reshape(2, ORBS, ORBS, 1, 64)


def solution(mesh):
    placed = (P("kpt", None), P("kpt", "freq", None), P(None, None, None, "freq", None), P(), P())
    return jax.shard_map(
        local,
        mesh=mesh,
        in_specs=placed,
        out_specs=P(None, None, None, ("freq", "kpt"), None),
        check_vma=False,
    )
```

time: 333 us -> 82.6 us (0.25)
  other arithmetic: 181 us -> 0 us
  Pallas kernels: 0 us -> 37.7 us
  local copies, waits for them, and re-layouts: 36.6 us -> 0 us
  matrix products: 35.2 us -> 0 us
  waiting for transfers between devices: 15.7 us -> 0 us
  starting transfers between devices: 8.45 us -> 0 us
  between operations: 4.84 us -> 0.01 us
    another operation x27 -> x0, other arithmetic: 176 us -> none  [the longest x11 58.6 us: local_block(): factor = jnp.linalg.cholesky(square)]
    pallas_call x0 -> x3, Pallas kernels: none -> 37.7 us  [the longest x1 34.3 us: local(): pl.pallas_call(main_kernel, out_shape=jax.ShapeDtypeStruct((ATOMS, LANES)...]
    another operation x33 -> x0, matrix products: 17.7 us -> none  [the longest x10 4.64 us: local_block(): solved = jax.scipy.linalg.cho_solve((factor, True), upper_rows.T)]
    dot_general x10 -> x0, matrix products: 17.5 us -> none  [the longest x1 4.57 us: local_block(): real_part = jnp.einsum('amb,aob->amo', turned, wide, precision=HIGH)]
    another operation x44 -> x0, local copies, waits for them, and re-layouts: 17 us -> none
    all_to_all x2 -> x0, waiting for transfers between devices: 15.7 us -> none  [the longest x1 13.7 us: copy_for_each(): return lax.all_to_all(copies, axis, split_axis=0, concat_axis=0, tiled=True)]
    all_to_all x2 -> x0, starting transfers between devices: 8.45 us -> none  [the longest x1 5.2 us: copy_for_each(): return lax.all_to_all(copies, axis, split_axis=0, concat_axis=0, tiled=True)]
    transpose x6 -> x0, local copies, waits for them, and re-layouts: 5.42 us -> none  [the longest x1 2.54 us: local_block(): jax.scipy.linalg.solve_triangular(lower, proj.astype(jnp.float32).T, lowe...]
  transfers between devices with their start and end apart: 2 -> 0, of which waited for: 2 -> 0; matrix products, arithmetic and copies ran while one was open for 1% -> 0% of each run, Pallas kernels for 0% -> 0%
where the time goes in v1:
time: 82.6 us; the launch traced here: 82.3 us
  blocking collectives  44.6 us (54%)
  Pallas kernels  37.7 us (46%)
    pallas_call x1, Pallas kernels, local(): pl.pallas_call(main_kernel, out_shape=jax.ShapeDtypeStruct((ATOMS, LANES)...  34.3 us
    all_to_all x1, blocking collectives, local(): lax.all_to_all(packed, 'freq', split_axis=0, concat_axis=0, tiled=True)  29.6 us
    all_to_all x1, blocking collectives, local(): lax.all_to_all(blocks.reshape(ATOMS, 1, LANES), ('freq', 'kpt'), split_ax...  15 us
    pallas_call x1, Pallas kernels, local(): pl.pallas_call(pack_kernel, out_shape=jax.ShapeDtypeStruct((64, 16, BANDS...  1.95 us

profile of v1, /device:TPU:1, one launch (start us, length us, event | category | flops | bytes accessed | tf_op | source)
XLA Modules:
  0.0 82.3 jit_solution(18070915004390612745)
XLA Ops:
  0.0 1.9 %pack.1 = bf16[64,16,384]{2,1,0:T(8,128)(2,1)} custom-call(bf16[10,384]{1,0:T(8,128)(2,1)} %bitcast.13, f32[50,2,64]{2,1,0:T(2,128)} %bitcast.12), custom_call_target="tpu_custom_call" | custom-call | tf_op jit(solution)/shard_map/pack/pallas_call | solution.py:224
  1.9 29.6 %all_to_all.10 = bf16[64,16,384]{2,1,0:T(8,128)(2,1)} all-to-all(bf16[64,16,384]{2,1,0:T(8,128)(2,1)} %pack.1), channel_id=1, replica_groups=mesh['freq'=64,'kpt'=2] {'freq'}, dimensions={0} | all-to-all | bytes 1572864 | tf_op jit(solution)/shard_map/all_to_all | solution.py:232
  31.5 34.3 %green.1 = f32[128,128]{1,0:T(8,128)} custom-call(bf16[1024,384]{1,0:T(8,128)(2,1)} %bitcast.9, s32[1,128]{1,0:T(1,128)} %bitcast.14, f32[1,384]{1,0:T(1,128)} %energy_ref.1, s32[2]{0:T(128)} %weight_ref.1), custom_call_target="tpu_custom_call" | custom-call | tf_op jit(solution)/shard_map/green/pallas_call | solution.py:233
  65.8 15.0 %all_to_all.11 = f32[128,1,128]{2,1,0:T(1,128)} all-to-all(f32[128,1,128]{2,1,0:T(1,128)} %bitcast.10), channel_id=1, replica_groups=mesh['freq'=64,'kpt'=2] {'freq','kpt'}, dimensions={0} | all-to-all | bytes 131072 | tf_op jit(solution)/shard_map/all_to_all | solution.py:246
  80.8 1.5 %unpack.1 = f32[50,1,64]{2,1,0:T(1,128)} custom-call(f32[128,128]{1,0:T(8,128)} %bitcast.11), custom_call_target="tpu_custom_call" | custom-call | tf_op jit(solution)/shard_map/unpack/pallas_call | solution.py:249

commit v2 on v1

--- a/solution.py
+++ b/solution.py
@@ -15,7 +15,7 @@
 LANES = 128
 CHUNKS = BANDS // LANES
 ROWS = 8
-PANELS = LANES // ROWS
+GROUP = 2
 
 f32 = jnp.float32
 bf16 = jnp.bfloat16
@@ -68,12 +68,14 @@
     return jnp.broadcast_to(x[:, i : i + 1], (ROWS, LANES))
 
 
-def sweep_panel(j, diag, rest, sub_iota, lane_iota):
-    first = ROWS * j
-    cols = [(lane_of(diag[0], first + t), lane_of(diag[1], first + t)) for t in range(ROWS)]
-    in_block = (lane_iota >= first) & (lane_iota < first + ROWS)
-    eye = jnp.where(lane_iota == sub_iota + first, 1.0, 0.0).astype(f32)
-    work = [(jnp.where(in_block, eye, diag[0]), jnp.where(in_block, 0.0, diag[1]))] + rest
+def sweep_panel(panel, first, sub_iota, lane_iota):
+    home, off = divmod(first, LANES)
+    diag = panel[home]
+    cols = [(lane_of(diag[0], off + t), lane_of(diag[1], off + t)) for t in range(ROWS)]
+    in_block = (lane_iota >= off) & (lane_iota < off + ROWS)
+    eye = jnp.where(lane_iota == sub_iota + off, 1.0, 0.0).astype(f32)
+    work = list(panel)
+    work[home] = (jnp.where(in_block, eye, diag[0]), jnp.where(in_block, 0.0, diag[1]))
     for p in range(0, ROWS, 2):
         q = p + 1
         ar, ai = row_of(cols[p][0], p), row_of(cols[p][1], p)
@@ -107,14 +109,32 @@
         for t in range(q + 1, ROWS):
             cols[t] = step(cols[t])
         work = [step(x) for x in work]
-    head_r, head_i = work[0]
-    update = [(jnp.where(in_block, eye - head_r, head_r), jnp.where(in_block, -head_i, head_i))] + work[1:]
-    final = [(jnp.where(in_block, -head_r, head_r), jnp.where(in_block, -head_i, head_i))] + work[1:]
+    head_r, head_i = work[home]
+    update, final = list(work), list(work)
+    update[home] = (jnp.where(in_block, eye - head_r, head_r), jnp.where(in_block, -head_i, head_i))
+    final[home] = (jnp.where(in_block, -head_r, head_r), jnp.where(in_block, -head_i, head_i))
     return update, final
 
 
-def stack_parts(top, bottom, order):
-    parts = split3(jnp.concatenate([top, bottom], axis=0))
+def apply_sweep(panel, update, first):
+    home, off = divmod(first, LANES)
+    out = list(panel)
+    cols = [
+        (lane_of(panel[home][0], off + t), lane_of(panel[home][1], off + t)) for t in range(ROWS)
+    ]
+    for c in range(CHUNKS):
+        xr, xi = out[c]
+        for t in range(ROWS):
+            cr, ci = cols[t]
+            ur, ui = row_of(update[c][0], t), row_of(update[c][1], t)
+            xr = xr - (cr * ur - ci * ui)
+            xi = xi - (cr * ui + ci * ur)
+        out[c] = (xr, xi)
+    return out
+
+
+def stack_parts(rows, order):
+    parts = split3(jnp.concatenate(rows, axis=0))
     return jnp.concatenate([parts[i] for i in order], axis=0)
 
 
@@ -166,32 +186,53 @@
     sub_iota = lax.broadcasted_iota(jnp.int32, (ROWS, LANES), 0)
     lane_iota = lax.broadcasted_iota(jnp.int32, (ROWS, LANES), 1)
 
-    def block_step(kb, carry):
-        chunk = [kb, lax.rem(kb + 1, CHUNKS), lax.rem(kb + 2, CHUNKS)]
-        for j in range(PANELS):
-            at = pl.ds(pl.multiple_of(kb * LANES + ROWS * j, ROWS), ROWS)
-            panel = [(re_ref[c, at, :], im_ref[c, at, :]) for c in chunk]
-            update, final = sweep_panel(j, panel[0], panel[1:], sub_iota, lane_iota)
-            left = jnp.concatenate(
-                [stack_parts(r, i, LEFT) for r, i in panel], axis=1
-            )
-            for z in range(CHUNKS):
+    def load(first):
+        return [(re_ref[c, first : first + ROWS, :], im_ref[c, first : first + ROWS, :]) for c in range(CHUNKS)]
+
+    def masked(panel, firsts):
+        out = []
+        for c in range(CHUNKS):
+            r, i = panel[c]
+            for first in firsts:
+                home, off = divmod(first, LANES)
+                if home == c:
+                    gone = (lane_iota >= off) & (lane_iota < off + ROWS)
+                    r, i = jnp.where(gone, 0.0, r), jnp.where(gone, 0.0, i)
+            out.append((r, i))
+        return out
+
+    window = [load(ROWS * g) for g in range(GROUP)]
+    for g in range(BANDS // (GROUP * ROWS)):
+        firsts = [ROWS * (GROUP * g + n) for n in range(GROUP)]
+        last = firsts[-1] + ROWS == BANDS
+        ahead = [] if last else [load(first + GROUP * ROWS) for first in firsts]
+        lefts, updates = [], []
+        for n in range(GROUP):
+            first = firsts[n]
+            update, final = sweep_panel(window[n], first, sub_iota, lane_iota)
+            for c in range(CHUNKS):
+                re_ref[c, first : first + ROWS, :] = final[c][0]
+                im_ref[c, first : first + ROWS, :] = final[c][1]
+            lefts.append(masked(window[n], firsts[n:]))
+            updates.append(update)
+            for m in range(n + 1, GROUP):
+                window[m] = apply_sweep(window[m], update, first)
+            ahead = [apply_sweep(panel, update, first) for panel in ahead]
+        window = ahead
+        left = jnp.concatenate(
+            [stack_parts([part for panel in lefts for part in panel[c]], LEFT) for c in range(CHUNKS)],
+            axis=1,
+        )
+        for z in range(CHUNKS):
+            rows_re, rows_im = [], []
+            for update in updates:
                 r, i = update[z]
-                right = stack_parts(
-                    jnp.concatenate([r, i], axis=1), jnp.concatenate([-i, r], axis=1), RIGHT
-                )
-                prod = lax.dot_general(left, right, (((0,), (0,)), ((), ())), preferred_element_type=f32)
-                for y in range(CHUNKS):
-                    here = pl.ds(pl.multiple_of(chunk[y] * LANES, LANES), LANES)
-                    piece = prod[LANES * y : LANES * (y + 1), :]
-                    re_ref[chunk[z], here, :] = re_ref[chunk[z], here, :] - piece[:, 0:LANES]
-                    im_ref[chunk[z], here, :] = im_ref[chunk[z], here, :] - piece[:, LANES:]
-            for z in range(CHUNKS):
-                re_ref[chunk[z], at, :] = final[z][0]
-                im_ref[chunk[z], at, :] = final[z][1]
-        return carry
-
-    lax.fori_loop(0, CHUNKS, block_step, 0)
+                rows_re += [r, -i]
+                rows_im += [i, r]
+            right = jnp.concatenate([stack_parts(rows_re, RIGHT), stack_parts(rows_im, RIGHT)], axis=1)
+            prod = lax.dot_general(left, right, (((0,), (0,)), ((), ())), preferred_element_type=f32)
+            re_ref[z, :, :] = re_ref[z, :, :] - prod[:, 0:LANES]
+            im_ref[z, :, :] = im_ref[z, :, :] - prod[:, LANES:]
 
     wide = []
     for ref in (re_ref, im_ref):

time: 82.6 us -> 73.2 us (0.89)
  Pallas kernels: 37.7 us -> 28.3 us
    pallas_call x1, Pallas kernels: 34.3 us -> 24.8 us  [local(): pl.pallas_call(main_kernel, out_shape=jax.ShapeDtypeStruct((ATOMS, LANES)...]
where the time goes in v2:
time: 73.2 us; the launch traced here: 72.9 us
  blocking collectives  44.6 us (61%)
  Pallas kernels  28.3 us (39%)
    all_to_all x1, blocking collectives, local(): lax.all_to_all(packed, 'freq', split_axis=0, concat_axis=0, tiled=True)  29.6 us
    pallas_call x1, Pallas kernels, local(): pl.pallas_call(main_kernel, out_shape=jax.ShapeDtypeStruct((ATOMS, LANES)...  24.8 us
    all_to_all x1, blocking collectives, local(): lax.all_to_all(blocks.reshape(ATOMS, 1, LANES), ('freq', 'kpt'), split_ax...  15 us
    pallas_call x1, Pallas kernels, local(): pl.pallas_call(pack_kernel, out_shape=jax.ShapeDtypeStruct((64, 16, BANDS...  1.95 us
    pallas_call x1, Pallas kernels, local(): pl.pallas_call(unpack_kernel, out_shape=jax.ShapeDtypeStruct((PARTS, 1, 6...  1.53 us

profile of v2, /device:TPU:1, one launch (start us, length us, event | category | flops | bytes accessed | tf_op | source)
XLA Modules:
  0.0 72.9 jit_solution(13975885320695474850)
XLA Ops:
  0.0 1.9 %pack.1 = bf16[64,16,384]{2,1,0:T(8,128)(2,1)} custom-call(bf16[10,384]{1,0:T(8,128)(2,1)} %bitcast.13, f32[50,2,64]{2,1,0:T(2,128)} %bitcast.12), custom_call_target="tpu_custom_call" | custom-call | tf_op jit(solution)/shard_map/pack/pallas_call | solution.py:265
  1.9 29.6 %all_to_all.10 = bf16[64,16,384]{2,1,0:T(8,128)(2,1)} all-to-all(bf16[64,16,384]{2,1,0:T(8,128)(2,1)} %pack.1), channel_id=1, replica_groups=mesh['freq'=64,'kpt'=2] {'freq'}, dimensions={0} | all-to-all | bytes 1572864 | tf_op jit(solution)/shard_map/all_to_all | solution.py:273
  31.5 24.8 %green.1 = f32[128,128]{1,0:T(8,128)} custom-call(bf16[1024,384]{1,0:T(8,128)(2,1)} %bitcast.9, s32[1,128]{1,0:T(1,128)} %bitcast.14, f32[1,384]{1,0:T(1,128)} %energy_ref.1, s32[2]{0:T(128)} %weight_ref.1), custom_call_target="tpu_custom_call" | custom-call | tf_op jit(solution)/shard_map/green/pallas_call | solution.py:274
  56.4 15.0 %all_to_all.11 = f32[128,1,128]{2,1,0:T(1,128)} all-to-all(f32[128,1,128]{2,1,0:T(1,128)} %bitcast.10), channel_id=1, replica_groups=mesh['freq'=64,'kpt'=2] {'freq','kpt'}, dimensions={0} | all-to-all | bytes 131072 | tf_op jit(solution)/shard_map/all_to_all | solution.py:287
  71.4 1.5 %unpack.1 = f32[50,1,64]{2,1,0:T(1,128)} custom-call(f32[128,128]{1,0:T(8,128)} %bitcast.11), custom_call_target="tpu_custom_call" | custom-call | tf_op jit(solution)/shard_map/unpack/pallas_call | solution.py:290

commit v3 on v2

--- a/solution.py
+++ b/solution.py
@@ -64,14 +64,14 @@
     return jnp.broadcast_to(x[i : i + 1, :], (ROWS, LANES))
 
 
-def lane_of(x, i):
-    return jnp.broadcast_to(x[:, i : i + 1], (ROWS, LANES))
-
-
-def sweep_panel(panel, first, sub_iota, lane_iota):
+def lane_of(x, i, zero):
+    return jnp.broadcast_to(x[:, i : i + 1], (ROWS, LANES)) + zero
+
+
+def sweep_panel(panel, first, sub_iota, lane_iota, zero):
     home, off = divmod(first, LANES)
     diag = panel[home]
-    cols = [(lane_of(diag[0], off + t), lane_of(diag[1], off + t)) for t in range(ROWS)]
+    cols = [(lane_of(diag[0], off + t, zero), lane_of(diag[1], off + t, zero)) for t in range(ROWS)]
     in_block = (lane_iota >= off) & (lane_iota < off + ROWS)
     eye = jnp.where(lane_iota == sub_iota + off, 1.0, 0.0).astype(f32)
     work = list(panel)
@@ -120,7 +120,8 @@
     home, off = divmod(first, LANES)
     out = list(panel)
     cols = [
-        (lane_of(panel[home][0], off + t), lane_of(panel[home][1], off + t)) for t in range(ROWS)
+        tuple(jnp.broadcast_to(part[:, off + t : off + t + 1], (ROWS, LANES)) for part in panel[home])
+        for t in range(ROWS)
     ]
     for c in range(CHUNKS):
         xr, xi = out[c]
@@ -185,6 +186,7 @@
 
     sub_iota = lax.broadcasted_iota(jnp.int32, (ROWS, LANES), 0)
     lane_iota = lax.broadcasted_iota(jnp.int32, (ROWS, LANES), 1)
+    zero = jnp.broadcast_to(energy_ref[:, 0:LANES] * 0.0, (ROWS, LANES))
 
     def load(first):
         return [(re_ref[c, first : first + ROWS, :], im_ref[c, first : first + ROWS, :]) for c in range(CHUNKS)]
@@ -209,7 +211,7 @@
         lefts, updates = [], []
         for n in range(GROUP):
             first = firsts[n]
-            update, final = sweep_panel(window[n], first, sub_iota, lane_iota)
+            update, final = sweep_panel(window[n], first, sub_iota, lane_iota, zero)
             for c in range(CHUNKS):
                 re_ref[c, first : first + ROWS, :] = final[c][0]
                 im_ref[c, first : first + ROWS, :] = final[c][1]
@@ -268,6 +270,7 @@
         in_specs=[vmem(), vmem()],
         out_specs=vmem(),
         scratch_shapes=[pltpu.VMEM((LANES, LANES), f32)],
+        compiler_params=pltpu.CompilerParams(vmem_limit_bytes=8 * 2**20),
         name="pack",
     )(projector.reshape(10, BANDS), sigma.reshape(PARTS, 2, 64))
     arrived = lax.all_to_all(packed, "freq", split_axis=0, concat_axis=0, tiled=True)
@@ -282,6 +285,7 @@
             pltpu.VMEM((2 * BANDS, 640), bf16),
             pltpu.VMEM((LANES, LANES), f32),
         ],
+        compiler_params=pltpu.CompilerParams(vmem_limit_bytes=24 * 2**20),
         name="green",
     )(arrived.reshape(1024, BANDS), atom_of_slot.reshape(1, ATOMS), band_energy, kweight)
     back = lax.all_to_all(
@@ -292,6 +296,7 @@
         out_shape=jax.ShapeDtypeStruct((PARTS, 1, 64), f32),
         in_specs=[vmem()],
         out_specs=vmem(),
+        compiler_params=pltpu.CompilerParams(vmem_limit_bytes=8 * 2**20),
         name="unpack",
     )(back.reshape(ATOMS, LANES))
     return out.reshape(2, ORBS, ORBS, 1, 64)

time: 73.2 us -> 66.9 us (0.914)
  Pallas kernels: 28.3 us -> 22.1 us
  blocking collectives: 44.6 us -> 42.4 us
  local copies, waits for them, and re-layouts: 0 us -> 2.19 us
    pallas_call x1, Pallas kernels: 24.8 us -> 21.2 us  [local(): pl.pallas_call(main_kernel, out_shape=jax.ShapeDtypeStruct((ATOMS, LANES)...]
    unnamed x0 -> x10, local copies, waits for them, and re-layouts: none -> 2.19 us
    all_to_all x1, blocking collectives: 15 us -> 13.1 us  [local(): lax.all_to_all(blocks.reshape(ATOMS, 1, LANES), ('freq', 'kpt'), split_ax...]
    pallas_call x1, Pallas kernels: 1.95 us -> 0.19 us  [local(): pl.pallas_call(pack_kernel, out_shape=jax.ShapeDtypeStruct((64, 16, BANDS...]
    pallas_call x1, Pallas kernels: 1.53 us -> 0.69 us  [local(): pl.pallas_call(unpack_kernel, out_shape=jax.ShapeDtypeStruct((PARTS, 1, 6...]
where the time goes in v3:
time: 66.9 us; the launch traced here: 66.7 us
  blocking collectives  42.4 us (63%)
  Pallas kernels  22.1 us (33%)
  local copies, waits for them, and re-layouts  2.19 us (3%)
    all_to_all x1, blocking collectives, local(): lax.all_to_all(packed, 'freq', split_axis=0, concat_axis=0, tiled=True)  29.3 us
    pallas_call x1, Pallas kernels, local(): pl.pallas_call(main_kernel, out_shape=jax.ShapeDtypeStruct((ATOMS, LANES)...  21.2 us
    all_to_all x1, blocking collectives, local(): lax.all_to_all(blocks.reshape(ATOMS, 1, LANES), ('freq', 'kpt'), split_ax...  13.1 us
    unnamed x10, local copies, waits for them, and re-layouts  2.19 us

profile of v3, /device:TPU:1, one launch (start us, length us, event | category | flops | bytes accessed | tf_op | source)
XLA Modules:
  0.0 66.7 jit_solution(17525464653546850822)
XLA Ops:
  0.0 0.0 copy-start
  0.0 0.8 %copy-done = f32[2,5,5,2,64]{4,3,2,1,0:T(2,128)S(1)} copy-done((f32[2,5,5,2,64]{4,3,2,1,0:T(2,128)S(1)}, f32[2,5,5,2,64]{4,3,2,1,0:T(2,128)}, u32[]{:S(2)}) %copy-start) | copy-done | bytes 25624
  0.8 0.0 copy-start.1
  0.8 0.7 %copy-done.1 = bf16[1,10,384]{2,1,0:T(8,128)(2,1)S(1)} copy-done((bf16[1,10,384]{2,1,0:T(8,128)(2,1)S(1)}, bf16[1,10,384]{2,1,0:T(8,128)(2,1)}, u32[]{:S(2)}) %copy-start.1) | copy-done | bytes 7704
  1.5 0.2 pack.1
  1.7 29.3 %all_to_all.10 = bf16[64,16,384]{2,1,0:T(8,128)(2,1)S(1)} all-to-all(bf16[64,16,384]{2,1,0:T(8,128)(2,1)S(1)} %pack.1), channel_id=1, replica_groups=mesh['freq'=64,'kpt'=2] {'freq'}, dimensions={0} | all-to-all | bytes 1572864 | tf_op jit(solution)/shard_map/all_to_all | solution.py:276
  31.0 0.0 copy-start.2
  31.0 0.0 copy-start.3
  31.0 0.0 copy-start.4
  31.0 0.7 %copy-done.2 = f32[1,384]{1,0:T(1,128)S(1)} copy-done((f32[1,384]{1,0:T(1,128)S(1)}, f32[1,384]{1,0:T(1,128)}, u32[]{:S(2)}) %copy-start.2) | copy-done | bytes 1560
  31.7 0.0 copy-done.3
  31.7 0.0 copy-done.4
  31.7 21.2 %green.1 = f32[128,128]{1,0:T(8,128)S(1)} custom-call(bf16[1024,384]{1,0:T(8,128)(2,1)S(1)} %bitcast.9, s32[1,128]{1,0:T(1,128)S(1)} %bitcast.14, f32[1,384]{1,0:T(1,128)S(1)} %copy-done.2, s32[2]{0:T(128)S(1)} %copy-done.4), custom_call_target="tpu_custom_call" | custom-call | tf_op jit(solution)/shard_map/green/pallas_call | solution.py:277
  52.9 13.1 %all_to_all.11 = f32[128,1,128]{2,1,0:T(1,128)S(1)} all-to-all(f32[128,1,128]{2,1,0:T(1,128)S(1)} %bitcast.10), channel_id=1, replica_groups=mesh['freq'=64,'kpt'=2] {'freq','kpt'}, dimensions={0} | all-to-all | bytes 131072 | tf_op jit(solution)/shard_map/all_to_all | solution.py:291
  66.0 0.7 %unpack.1 = f32[50,1,64]{2,1,0:T(1,128)} custom-call(f32[128,128]{1,0:T(8,128)S(1)} %bitcast.11), custom_call_target="tpu_custom_call" | custom-call | tf_op jit(solution)/shard_map/unpack/pallas_call | solution.py:294
Async XLA Ops:
  0.0 0.8 %copy-start = (f32[2,5,5,2,64]{4,3,2,1,0:T(2,128)S(1)}, f32[2,5,5,2,64]{4,3,2,1,0:T(2,128)}, u32[]{:S(2)}) copy-start(f32[2,5,5,2,64]{4,3,2,1,0:T(2,128)} %param.7) | copy-start | bytes 76804
  0.8 0.7 %copy-start.1 = (bf16[1,10,384]{2,1,0:T(8,128)(2,1)S(1)}, bf16[1,10,384]{2,1,0:T(8,128)(2,1)}, u32[]{:S(2)}) copy-start(bf16[1,10,384]{2,1,0:T(8,128)(2,1)} %param.6) | copy-start | bytes 23044
  31.0 0.7 %copy-start.2 = (f32[1,384]{1,0:T(1,128)S(1)}, f32[1,384]{1,0:T(1,128)}, u32[]{:S(2)}) copy-start(f32[1,384]{1,0:T(1,128)} %energy_ref.1) | copy-start | bytes 4612
  31.0 0.7 %copy-start.3 = (s32[128]{0:T(128)S(1)}, s32[128]{0:T(128)}, u32[]{:S(2)}) copy-start(s32[128]{0:T(128)} %param.8) | copy-start | bytes 1540
  31.0 0.7 %copy-start.4 = (s32[2]{0:T(128)S(1)}, s32[2]{0:T(128)}, u32[]{:S(2)}) copy-start(s32[2]{0:T(128)} %weight_ref.1) | copy-start | bytes 28

commit v4 on v1

--- a/solution.py
+++ b/solution.py
@@ -15,7 +15,8 @@
 LANES = 128
 CHUNKS = BANDS // LANES
 ROWS = 8
-PANELS = LANES // ROWS
+GROUP = 2
+PAIRS = 15
 
 f32 = jnp.float32
 bf16 = jnp.bfloat16
@@ -64,16 +65,15 @@
     return jnp.broadcast_to(x[i : i + 1, :], (ROWS, LANES))
 
 
-def lane_of(x, i):
-    return jnp.broadcast_to(x[:, i : i + 1], (ROWS, LANES))
-
-
-def sweep_panel(j, diag, rest, sub_iota, lane_iota):
-    first = ROWS * j
-    cols = [(lane_of(diag[0], first + t), lane_of(diag[1], first + t)) for t in range(ROWS)]
-    in_block = (lane_iota >= first) & (lane_iota < first + ROWS)
-    eye = jnp.where(lane_iota == sub_iota + first, 1.0, 0.0).astype(f32)
-    work = [(jnp.where(in_block, eye, diag[0]), jnp.where(in_block, 0.0, diag[1]))] + rest
+def lane_of(x, i, zero):
+    return jnp.broadcast_to(x[:, i : i + 1], (ROWS, LANES)) + zero
+
+
+def sweep_panel(panel, off, sub_iota, lane_iota, zero):
+    cols = [(lane_of(panel[0], off + t, zero), lane_of(panel[1], off + t, zero)) for t in range(ROWS)]
+    in_block = (lane_iota >= off) & (lane_iota < off + ROWS)
+    eye = jnp.where(lane_iota == sub_iota + off, 1.0, 0.0).astype(f32)
+    work = (jnp.where(in_block, eye, panel[0]), jnp.where(in_block, 0.0, panel[1]))
     for p in range(0, ROWS, 2):
         q = p + 1
         ar, ai = row_of(cols[p][0], p), row_of(cols[p][1], p)
@@ -106,23 +106,126 @@
 
         for t in range(q + 1, ROWS):
             cols[t] = step(cols[t])
-        work = [step(x) for x in work]
-    head_r, head_i = work[0]
-    update = [(jnp.where(in_block, eye - head_r, head_r), jnp.where(in_block, -head_i, head_i))] + work[1:]
-    final = [(jnp.where(in_block, -head_r, head_r), jnp.where(in_block, -head_i, head_i))] + work[1:]
+        work = step(work)
+    re, im = work
+    update = (jnp.where(in_block, eye - re, re), jnp.where(in_block, -im, im))
+    final = (jnp.where(in_block, -re, re), jnp.where(in_block, -im, im))
     return update, final
 
 
-def stack_parts(top, bottom, order):
-    parts = split3(jnp.concatenate([top, bottom], axis=0))
-    return jnp.concatenate([parts[i] for i in order], axis=0)
-
-
-LEFT = (0, 0, 0, 1, 1, 2)
-RIGHT = (0, 1, 2, 0, 1, 0)
-
-
-def main_kernel(buf_ref, atom_ref, energy_ref, weight_ref, out_ref, re_ref, im_ref, rows_ref, out_tmp):
+def apply_sweep(panel, update, off):
+    xr, xi = panel
+    sum_r, sum_i = [], []
+    for t in range(ROWS):
+        cr = jnp.broadcast_to(panel[0][:, off + t : off + t + 1], (ROWS, LANES))
+        ci = jnp.broadcast_to(panel[1][:, off + t : off + t + 1], (ROWS, LANES))
+        ur, ui = row_of(update[0], t), row_of(update[1], t)
+        pr, pi = cmul(cr, ci, ur, ui)
+        sum_r.append(pr)
+        sum_i.append(pi)
+    return xr - tree(sum_r), xi - tree(sum_i)
+
+
+def tree(terms):
+    while len(terms) > 1:
+        terms = [sum(terms[i : i + 2][1:], terms[i]) for i in range(0, len(terms), 2)]
+    return terms[0]
+
+
+LEFT = (0, 0, 1)
+RIGHT = (0, 1, 0)
+
+
+def cat(parts, axis):
+    return jnp.concatenate(parts, axis=axis)
+
+
+def dot(a, b):
+    return jnp.dot(a, b, preferred_element_type=f32)
+
+
+def stack_parts(rows, order):
+    parts = split3(cat(rows, 0))
+    return cat([parts[i] for i in order], 0)
+
+
+def mul_wide(a, b):
+    ar, ai = split3(a[0]), split3(a[1])
+    br, bi, bn = split3(b[0]), split3(b[1]), split3(-b[1])
+    left = cat([x for i in LEFT for x in (ar[i], ai[i])], 1)
+    right = cat([cat([cat([br[i], bi[i]], 1), cat([bn[i], br[i]], 1)], 0) for i in RIGHT], 0)
+    out = dot(left, right)
+    n = b[0].shape[1]
+    return out[:, 0:n], out[:, n:]
+
+
+def mul_tall(a, b):
+    ar, ai, an = split3(a[0]), split3(a[1]), split3(-a[1])
+    br, bi = split3(b[0]), split3(b[1])
+    left = cat([cat([cat([ar[i], an[i]], 1), cat([ai[i], ar[i]], 1)], 0) for i in LEFT], 1)
+    right = cat([x for i in RIGHT for x in (br[i], bi[i])], 0)
+    out = dot(left, right)
+    m = a[0].shape[0]
+    return out[0:m, :], out[m:, :]
+
+
+def mul_real(a, exact):
+    left = cat(split3(cat([a[0], a[1]], 0)), 1)
+    out = dot(left, cat([exact] * 3, 0))
+    m = a[0].shape[0]
+    return out[0:m, :], out[m:, :]
+
+
+def add(x, y):
+    return x[0] + y[0], x[1] + y[1]
+
+
+def sweep_block(re_ref, im_ref, k, sub_iota, lane_iota, zero):
+    def load(off):
+        return re_ref[k, off : off + ROWS, :], im_ref[k, off : off + ROWS, :]
+
+    def masked(panel, off, stop):
+        gone = (lane_iota >= off) & (lane_iota < stop)
+        return jnp.where(gone, 0.0, panel[0]), jnp.where(gone, 0.0, panel[1])
+
+    span = GROUP * ROWS
+    window = [load(ROWS * n) for n in range(GROUP)]
+    for base in range(0, LANES, span):
+        follow = base + span
+        ahead = load(follow) if follow < LANES else None
+        lefts, updates = [], []
+        for n in range(GROUP):
+            off = base + ROWS * n
+            update, final = sweep_panel(window[n], off, sub_iota, lane_iota, zero)
+            re_ref[k, off : off + ROWS, :] = final[0]
+            im_ref[k, off : off + ROWS, :] = final[1]
+            lefts.append(masked(window[n], off, follow))
+            updates.append(update)
+            for m in range(n + 1, GROUP):
+                window[m] = apply_sweep(window[m], update, off)
+            if ahead is not None:
+                ahead = apply_sweep(ahead, update, off)
+        left = stack_parts([x for panel in lefts for x in panel], LEFT).T
+        right = cat(
+            [
+                stack_parts([x for r, i in updates for x in (r, -i)], RIGHT),
+                stack_parts([x for r, i in updates for x in (i, r)], RIGHT),
+            ],
+            1,
+        )
+        if ahead is not None:
+            early = dot(left[follow : follow + span, :], right)
+            window = [ahead]
+            for n in range(1, GROUP):
+                at = slice(ROWS * n, ROWS * (n + 1))
+                r, i = load(follow + ROWS * n)
+                window.append((r - early[at, 0:LANES], i - early[at, LANES:]))
+        prod = dot(left, right)
+        re_ref[k, :, :] = re_ref[k, :, :] - prod[:, 0:LANES]
+        im_ref[k, :, :] = im_ref[k, :, :] - prod[:, LANES:]
+
+
+def main_kernel(buf_ref, atom_ref, energy_ref, weight_ref, out_ref, re_ref, im_ref, pt_ref, rows_ref, acc_ref, out_tmp):
     freq = lax.axis_index("freq")
     kpt = lax.axis_index("kpt")
     omega = (2.0 * freq.astype(f32) + 1.0) * math.pi * BETA_INV
@@ -142,7 +245,8 @@
     odd = (lax.broadcasted_iota(jnp.int32, (64, LANES), 1) & 1) == 1
     sig = jnp.where(odd, sig_parts[64:128, :], sig_parts[0:64, :])
 
-    proj_b = turned[:, 0:640].astype(bf16)
+    pt_ref[...] = turned[:, 0:640].astype(bf16)
+    proj_b = pt_ref[...]
     for x in range(2):
         for m in range(ORBS):
             acc = None
@@ -159,60 +263,64 @@
     jj = lax.broadcasted_iota(jnp.int32, (BANDS, BANDS), 1)
     x_mat = jnp.where(ii == jj, -energy_ref[...], 0.0) - 0.5 * (up_r + up_r.T)
     y_mat = jnp.where(ii == jj, omega, 0.0) - 0.5 * (up_i + up_i.T)
-    for c in range(CHUNKS):
-        re_ref[c, :, :] = x_mat[:, LANES * c : LANES * (c + 1)]
-        im_ref[c, :, :] = y_mat[:, LANES * c : LANES * (c + 1)]
+
+    def block(i, j):
+        at = (slice(LANES * i, LANES * (i + 1)), slice(LANES * j, LANES * (j + 1)))
+        return x_mat[at], y_mat[at]
 
     sub_iota = lax.broadcasted_iota(jnp.int32, (ROWS, LANES), 0)
     lane_iota = lax.broadcasted_iota(jnp.int32, (ROWS, LANES), 1)
-
-    def block_step(kb, carry):
-        chunk = [kb, lax.rem(kb + 1, CHUNKS), lax.rem(kb + 2, CHUNKS)]
-        for j in range(PANELS):
-            at = pl.ds(pl.multiple_of(kb * LANES + ROWS * j, ROWS), ROWS)
-            panel = [(re_ref[c, at, :], im_ref[c, at, :]) for c in chunk]
-            update, final = sweep_panel(j, panel[0], panel[1:], sub_iota, lane_iota)
-            left = jnp.concatenate(
-                [stack_parts(r, i, LEFT) for r, i in panel], axis=1
-            )
-            for z in range(CHUNKS):
-                r, i = update[z]
-                right = stack_parts(
-                    jnp.concatenate([r, i], axis=1), jnp.concatenate([-i, r], axis=1), RIGHT
-                )
-                prod = lax.dot_general(left, right, (((0,), (0,)), ((), ())), preferred_element_type=f32)
-                for y in range(CHUNKS):
-                    here = pl.ds(pl.multiple_of(chunk[y] * LANES, LANES), LANES)
-                    piece = prod[LANES * y : LANES * (y + 1), :]
-                    re_ref[chunk[z], here, :] = re_ref[chunk[z], here, :] - piece[:, 0:LANES]
-                    im_ref[chunk[z], here, :] = im_ref[chunk[z], here, :] - piece[:, LANES:]
-            for z in range(CHUNKS):
-                re_ref[chunk[z], at, :] = final[z][0]
-                im_ref[chunk[z], at, :] = final[z][1]
-        return carry
-
-    lax.fori_loop(0, CHUNKS, block_step, 0)
-
-    wide = []
-    for ref in (re_ref, im_ref):
-        full = jnp.concatenate([ref[c, :, :] for c in range(CHUNKS)], axis=1)
-        hi = full.astype(bf16)
-        low = (full - hi.astype(f32)).astype(bf16)
-        wide.append(jnp.concatenate([hi, low], axis=1))
-    left = jnp.concatenate(wide, axis=0)
-    twice = jnp.concatenate([proj_b, proj_b], axis=0)
-    gp = lax.dot_general(left, twice, (((1,), (0,)), ((), ())), preferred_element_type=f32)
+    zero = jnp.broadcast_to(energy_ref[:, 0:LANES] * 0.0, (ROWS, LANES))
+
+    blocks = {(i, j): block(i, j) for i in range(CHUNKS) for j in range(CHUNKS)}
+    exact = pt_ref[0:LANES, :]
+    for k in range(CHUNKS):
+        re_ref[k, :, :], im_ref[k, :, :] = blocks[k, k]
+        sweep_block(re_ref, im_ref, k, sub_iota, lane_iota, zero)
+        swept = re_ref[k, :, :], im_ref[k, :, :]
+        after = range(k + 1, CHUNKS)
+        stack = [swept]
+        if k + 1 < CHUNKS:
+            below = tuple(cat([blocks[i, k][x] for i in after], 0) for x in range(2))
+            low = mul_wide(below, swept)
+            for j in after:
+                change = mul_wide(low, blocks[k, j])
+                for i in after:
+                    at = slice(LANES * (i - k - 1), LANES * (i - k))
+                    blocks[i, j] = add(blocks[i, j], (change[0][at, :], change[1][at, :]))
+            stack.append(low)
+        lhs = tuple(cat([part[x] for part in stack], 0) for x in range(2))
+        wide = mul_real(lhs, exact) if k == 0 else mul_tall(lhs, y[k])
+        z = wide[0][0:LANES, :], wide[1][0:LANES, :]
+        if k == 0:
+            y = [[pt_ref[LANES * i : LANES * (i + 1), :].astype(f32), None] for i in range(CHUNKS)]
+        for i in after:
+            at = slice(LANES * (i - k), LANES * (i - k + 1))
+            y[i] = [y[i][0] + wide[0][at, :], wide[1][at, :] if y[i][1] is None else y[i][1] + wide[1][at, :]]
+        n = 0
+        for m in range(ORBS):
+            for o in range(m, ORBS):
+                lm, lo = slice(LANES * m, LANES * (m + 1)), slice(LANES * o, LANES * (o + 1))
+                re, im = y[k][0][:, lm] * z[0][:, lo], y[k][0][:, lm] * z[1][:, lo]
+                if y[k][1] is not None:
+                    re = re - y[k][1][:, lm] * z[1][:, lo]
+                    im = im + y[k][1][:, lm] * z[0][:, lo]
+                for x, val in ((0, re), (1, im)):
+                    val = tree([val[ROWS * r : ROWS * (r + 1), :] for r in range(LANES // ROWS)])
+                    at = slice(ROWS * (x * PAIRS + n), ROWS * (x * PAIRS + n + 1))
+                    acc_ref[at, :] = val if k == 0 else acc_ref[at, :] + val
+                n += 1
     scale = -own / total
     out_tmp[...] = jnp.zeros_like(out_tmp)
     for x in range(2):
+        n = 0
         for m in range(ORBS):
-            v = gp[x * BANDS : (x + 1) * BANDS, LANES * m : LANES * (m + 1)]
             for o in range(m, ORBS):
-                val = jnp.sum(v * proj_t[o], axis=0, keepdims=True) * scale
-                i1, i2 = x * 25 + m * 5 + o, x * 25 + o * 5 + m
-                out_tmp[i1 : i1 + 1, :] = val
-                if o != m:
-                    out_tmp[i2 : i2 + 1, :] = val
+                at = slice(ROWS * (x * PAIRS + n), ROWS * (x * PAIRS + n + 1))
+                val = jnp.sum(acc_ref[at, :], axis=0, keepdims=True) * scale
+                n += 1
+                for i in {x * 25 + m * 5 + o, x * 25 + o * 5 + m}:
+                    out_tmp[i : i + 1, :] = val
     out_ref[...] = out_tmp[...].T
 
 
@@ -227,6 +335,7 @@
         in_specs=[vmem(), vmem()],
         out_specs=vmem(),
         scratch_shapes=[pltpu.VMEM((LANES, LANES), f32)],
+        compiler_params=pltpu.CompilerParams(vmem_limit_bytes=8 * 2**20),
         name="pack",
     )(projector.reshape(10, BANDS), sigma.reshape(PARTS, 2, 64))
     arrived = lax.all_to_all(packed, "freq", split_axis=0, concat_axis=0, tiled=True)
@@ -236,11 +345,14 @@
         in_specs=[vmem(), vmem(), vmem(), pl.BlockSpec(memory_space=pltpu.SMEM)],
         out_specs=vmem(),
         scratch_shapes=[
-            pltpu.VMEM((CHUNKS, BANDS, LANES), f32),
-            pltpu.VMEM((CHUNKS, BANDS, LANES), f32),
+            pltpu.VMEM((CHUNKS, LANES, LANES), f32),
+            pltpu.VMEM((CHUNKS, LANES, LANES), f32),
+            pltpu.VMEM((BANDS, 640), bf16),
             pltpu.VMEM((2 * BANDS, 640), bf16),
+            pltpu.VMEM((2 * PAIRS * ROWS, LANES), f32),
             pltpu.VMEM((LANES, LANES), f32),
         ],
+        compiler_params=pltpu.CompilerParams(vmem_limit_bytes=24 * 2**20),
         name="green",
     )(arrived.reshape(1024, BANDS), atom_of_slot.reshape(1, ATOMS), band_energy, kweight)
     back = lax.all_to_all(
@@ -251,6 +363,7 @@
         out_shape=jax.ShapeDtypeStruct((PARTS, 1, 64), f32),
         in_specs=[vmem()],
         out_specs=vmem(),
+        compiler_params=pltpu.CompilerParams(vmem_limit_bytes=8 * 2**20),
         name="unpack",
     )(back.reshape(ATOMS, LANES))
     return out.reshape(2, ORBS, ORBS, 1, 64)

time: 82.6 us -> 62.9 us (0.76)
  Pallas kernels: 37.7 us -> 18 us
  blocking collectives: 44.6 us -> 42.4 us
  local copies, waits for them, and re-layouts: 0 us -> 2.19 us
    pallas_call x1, Pallas kernels: 34.3 us -> 17.2 us  [local(): pl.pallas_call(main_kernel, out_shape=jax.ShapeDtypeStruct((ATOMS, LANES)...]
    unnamed x0 -> x10, local copies, waits for them, and re-layouts: none -> 2.19 us
    all_to_all x1, blocking collectives: 15 us -> 13.1 us  [local(): lax.all_to_all(blocks.reshape(ATOMS, 1, LANES), ('freq', 'kpt'), split_ax...]
    pallas_call x1, Pallas kernels: 1.95 us -> 0.19 us  [local(): pl.pallas_call(pack_kernel, out_shape=jax.ShapeDtypeStruct((64, 16, BANDS...]
    pallas_call x1, Pallas kernels: 1.53 us -> 0.69 us  [local(): pl.pallas_call(unpack_kernel, out_shape=jax.ShapeDtypeStruct((PARTS, 1, 6...]
where the time goes in v4:
time: 62.9 us; the launch traced here: 62.6 us
  blocking collectives  42.4 us (67%)
  Pallas kernels  18 us (29%)
  local copies, waits for them, and re-layouts  2.19 us (3%)
    all_to_all x1, blocking collectives, local(): lax.all_to_all(packed, 'freq', split_axis=0, concat_axis=0, tiled=True)  29.3 us
    pallas_call x1, Pallas kernels, local(): pl.pallas_call(main_kernel, out_shape=jax.ShapeDtypeStruct((ATOMS, LANES)...  17.2 us
    all_to_all x1, blocking collectives, local(): lax.all_to_all(blocks.reshape(ATOMS, 1, LANES), ('freq', 'kpt'), split_ax...  13.1 us
    unnamed x10, local copies, waits for them, and re-layouts  2.19 us

profile of v4, /device:TPU:1, one launch (start us, length us, event | category | flops | bytes accessed | tf_op | source)
XLA Modules:
  0.0 62.6 jit_solution(62611053339103672)
XLA Ops:
  0.0 0.0 copy-start
  0.0 0.8 %copy-done = f32[2,5,5,2,64]{4,3,2,1,0:T(2,128)S(1)} copy-done((f32[2,5,5,2,64]{4,3,2,1,0:T(2,128)S(1)}, f32[2,5,5,2,64]{4,3,2,1,0:T(2,128)}, u32[]{:S(2)}) %copy-start) | copy-done | bytes 25624
  0.8 0.0 copy-start.1
  0.8 0.7 %copy-done.1 = bf16[1,10,384]{2,1,0:T(8,128)(2,1)S(1)} copy-done((bf16[1,10,384]{2,1,0:T(8,128)(2,1)S(1)}, bf16[1,10,384]{2,1,0:T(8,128)(2,1)}, u32[]{:S(2)}) %copy-start.1) | copy-done | bytes 7704
  1.5 0.2 pack.1
  1.7 29.3 %all_to_all.10 = bf16[64,16,384]{2,1,0:T(8,128)(2,1)S(1)} all-to-all(bf16[64,16,384]{2,1,0:T(8,128)(2,1)S(1)} %pack.1), channel_id=1, replica_groups=mesh['freq'=64,'kpt'=2] {'freq'}, dimensions={0} | all-to-all | bytes 1572864 | tf_op jit(solution)/shard_map/all_to_all | solution.py:341
  31.0 0.0 copy-start.2
  31.0 0.0 copy-start.3
  31.0 0.0 copy-start.4
  31.0 0.7 %copy-done.2 = f32[1,384]{1,0:T(1,128)S(1)} copy-done((f32[1,384]{1,0:T(1,128)S(1)}, f32[1,384]{1,0:T(1,128)}, u32[]{:S(2)}) %copy-start.2) | copy-done | bytes 1560
  31.7 0.0 copy-done.3
  31.7 0.0 copy-done.4
  31.7 17.2 %green.1 = f32[128,128]{1,0:T(8,128)S(1)} custom-call(bf16[1024,384]{1,0:T(8,128)(2,1)S(1)} %bitcast.9, s32[1,128]{1,0:T(1,128)S(1)} %bitcast.14, f32[1,384]{1,0:T(1,128)S(1)} %copy-done.2, s32[2]{0:T(128)S(1)} %copy-done.4), custom_call_target="tpu_custom_call" | custom-call | tf_op jit(solution)/shard_map/green/pallas_call | solution.py:342
  48.8 13.1 %all_to_all.11 = f32[128,1,128]{2,1,0:T(1,128)S(1)} all-to-all(f32[128,1,128]{2,1,0:T(1,128)S(1)} %bitcast.10), channel_id=1, replica_groups=mesh['freq'=64,'kpt'=2] {'freq','kpt'}, dimensions={0} | all-to-all | bytes 131072 | tf_op jit(solution)/shard_map/all_to_all | solution.py:358
  61.9 0.7 %unpack.1 = f32[50,1,64]{2,1,0:T(1,128)} custom-call(f32[128,128]{1,0:T(8,128)S(1)} %bitcast.11), custom_call_target="tpu_custom_call" | custom-call | tf_op jit(solution)/shard_map/unpack/pallas_call | solution.py:361
Async XLA Ops:
  0.0 0.8 %copy-start = (f32[2,5,5,2,64]{4,3,2,1,0:T(2,128)S(1)}, f32[2,5,5,2,64]{4,3,2,1,0:T(2,128)}, u32[]{:S(2)}) copy-start(f32[2,5,5,2,64]{4,3,2,1,0:T(2,128)} %param.7) | copy-start | bytes 76804
  0.8 0.7 %copy-start.1 = (bf16[1,10,384]{2,1,0:T(8,128)(2,1)S(1)}, bf16[1,10,384]{2,1,0:T(8,128)(2,1)}, u32[]{:S(2)}) copy-start(bf16[1,10,384]{2,1,0:T(8,128)(2,1)} %param.6) | copy-start | bytes 23044
  31.0 0.7 %copy-start.2 = (f32[1,384]{1,0:T(1,128)S(1)}, f32[1,384]{1,0:T(1,128)}, u32[]{:S(2)}) copy-start(f32[1,384]{1,0:T(1,128)} %energy_ref.1) | copy-start | bytes 4612
  31.0 0.7 %copy-start.3 = (s32[128]{0:T(128)S(1)}, s32[128]{0:T(128)}, u32[]{:S(2)}) copy-start(s32[128]{0:T(128)} %param.8) | copy-start | bytes 1540
  31.0 0.7 %copy-start.4 = (s32[2]{0:T(128)S(1)}, s32[2]{0:T(128)}, u32[]{:S(2)}) copy-start(s32[2]{0:T(128)} %weight_ref.1) | copy-start | bytes 28

commit v5 on v4

--- a/solution.py
+++ b/solution.py
@@ -30,7 +30,23 @@
     return hi, mid, low
 
 
-def pack_kernel(proj_ref, sig_ref, out_ref, tmp_ref):
+def pack_kernel(
+    proj_hbm, sig_hbm, atom_hbm, energy_hbm, weight_hbm,
+    out_ref, atom_ref, energy_ref, scale_ref,
+    proj_ref, sig_ref, weight_ref, tmp_ref, sems,
+):
+    pairs = (
+        (sig_hbm, sig_ref), (proj_hbm, proj_ref), (atom_hbm, atom_ref),
+        (energy_hbm, energy_ref), (weight_hbm, weight_ref),
+    )
+    copies = [pltpu.make_async_copy(src, dst, sems.at[i]) for i, (src, dst) in enumerate(pairs)]
+    for copy in copies:
+        copy.start()
+    for copy in copies:
+        copy.wait()
+    total = (weight_ref[0] + weight_ref[1]).astype(f32)
+    own = jnp.where(lax.axis_index("kpt") == 0, weight_ref[0], weight_ref[1]).astype(f32)
+    scale_ref[...] = jnp.full((1, LANES), -own, f32) / jnp.full((1, LANES), total, f32)
     tmp_ref[...] = jnp.zeros_like(tmp_ref)
     tmp_ref[0:PARTS, 0:64] = sig_ref[:, 0, :]
     tmp_ref[64 : 64 + PARTS, 0:64] = sig_ref[:, 1, :]
@@ -225,12 +241,9 @@
         im_ref[k, :, :] = im_ref[k, :, :] - prod[:, LANES:]
 
 
-def main_kernel(buf_ref, atom_ref, energy_ref, weight_ref, out_ref, re_ref, im_ref, pt_ref, rows_ref, acc_ref, out_tmp):
+def main_kernel(buf_ref, atom_ref, energy_ref, scale_ref, out_ref, re_ref, im_ref, pt_ref, rows_ref, acc_ref, out_tmp):
     freq = lax.axis_index("freq")
-    kpt = lax.axis_index("kpt")
     omega = (2.0 * freq.astype(f32) + 1.0) * math.pi * BETA_INV
-    total = (weight_ref[0] + weight_ref[1]).astype(f32)
-    own = jnp.where(kpt == 0, weight_ref[0], weight_ref[1]).astype(f32)
 
     atom = atom_ref[...]
     base = (atom >> 1) * 16 + (atom & 1) * 5
@@ -310,7 +323,7 @@
                     at = slice(ROWS * (x * PAIRS + n), ROWS * (x * PAIRS + n + 1))
                     acc_ref[at, :] = val if k == 0 else acc_ref[at, :] + val
                 n += 1
-    scale = -own / total
+    scale = scale_ref[...]
     out_tmp[...] = jnp.zeros_like(out_tmp)
     for x in range(2):
         n = 0
@@ -329,20 +342,40 @@
 
 
 def local(band_energy, projector, sigma, atom_of_slot, kweight):
-    packed = pl.pallas_call(
+    anywhere = pl.BlockSpec(memory_space=pltpu.HBM)
+    packed, atom, energy, scale = pl.pallas_call(
         pack_kernel,
-        out_shape=jax.ShapeDtypeStruct((64, 16, BANDS), bf16),
-        in_specs=[vmem(), vmem()],
-        out_specs=vmem(),
-        scratch_shapes=[pltpu.VMEM((LANES, LANES), f32)],
+        out_shape=(
+            jax.ShapeDtypeStruct((64, 16, BANDS), bf16),
+            jax.ShapeDtypeStruct((1, ATOMS), jnp.int32),
+            jax.ShapeDtypeStruct((1, BANDS), f32),
+            jax.ShapeDtypeStruct((1, LANES), f32),
+        ),
+        in_specs=[anywhere] * 5,
+        out_specs=(vmem(),) * 4,
+        scratch_shapes=[
+            pltpu.VMEM((10, BANDS), bf16),
+            pltpu.VMEM((PARTS, 2, 64), f32),
+            pltpu.SMEM((2,), jnp.int32),
+            pltpu.VMEM((LANES, LANES), f32),
+            pltpu.SemaphoreType.DMA((5,)),
+        ],
         compiler_params=pltpu.CompilerParams(vmem_limit_bytes=8 * 2**20),
         name="pack",
-    )(projector.reshape(10, BANDS), sigma.reshape(PARTS, 2, 64))
+    )(
+        *(
+            pltpu.with_memory_space_constraint(x, pltpu.HBM)
+            for x in (
+                projector.reshape(10, BANDS), sigma.reshape(PARTS, 2, 64), atom_of_slot.reshape(1, ATOMS),
+                band_energy, kweight,
+            )
+        )
+    )
     arrived = lax.all_to_all(packed, "freq", split_axis=0, concat_axis=0, tiled=True)
     blocks = pl.pallas_call(
         main_kernel,
         out_shape=jax.ShapeDtypeStruct((ATOMS, LANES), f32),
-        in_specs=[vmem(), vmem(), vmem(), pl.BlockSpec(memory_space=pltpu.SMEM)],
+        in_specs=[vmem()] * 4,
         out_specs=vmem(),
         scratch_shapes=[
             pltpu.VMEM((CHUNKS, LANES, LANES), f32),
@@ -354,7 +387,7 @@
         ],
         compiler_params=pltpu.CompilerParams(vmem_limit_bytes=24 * 2**20),
         name="green",
-    )(arrived.reshape(1024, BANDS), atom_of_slot.reshape(1, ATOMS), band_energy, kweight)
+    )(arrived.reshape(1024, BANDS), atom, energy, scale)
     back = lax.all_to_all(
         blocks.reshape(ATOMS, 1, LANES), ("freq", "kpt"), split_axis=0, concat_axis=0, tiled=True
     )

time: 62.9 us -> 61 us (0.970)
  local copies, waits for them, and re-layouts: 2.19 us -> 0 us
    unnamed x10 -> x0, local copies, waits for them, and re-layouts: 2.19 us -> none
    pallas_call x1, Pallas kernels: 0.19 us -> 1.08 us  [local(): pl.pallas_call(pack_kernel, out_shape=(jax.ShapeDtypeStruct((64, 16, BAND...]
where the time goes in v5:
time: 61 us; the launch traced here: 60.8 us
  blocking collectives  42.4 us (70%)
  Pallas kernels  18.4 us (30%)
    all_to_all x1, blocking collectives, local(): lax.all_to_all(packed, 'freq', split_axis=0, concat_axis=0, tiled=True)  29.3 us
    pallas_call x1, Pallas kernels, local(): pl.pallas_call(main_kernel, out_shape=jax.ShapeDtypeStruct((ATOMS, LANES)...  16.6 us
    all_to_all x1, blocking collectives, local(): lax.all_to_all(blocks.reshape(ATOMS, 1, LANES), ('freq', 'kpt'), split_ax...  13.1 us

profile of v5, /device:TPU:1, one launch (start us, length us, event | category | flops | bytes accessed | tf_op | source)
XLA Modules:
  0.0 60.8 jit_solution(13022659402658476733)
XLA Ops:
  0.0 1.1 %pack.1 = (bf16[64,16,384]{2,1,0:T(8,128)(2,1)S(1)}, s32[1,128]{1,0:T(1,128)S(1)}, f32[1,384]{1,0:T(1,128)S(1)}, f32[1,128]{1,0:T(1,128)S(1)}) custom-call(bf16[10,384]{1,0:T(8,128)(2,1)} %bitcast.13, f32[50,2,64]{2,1,0:T(2,128)} %bitcast.12, s32[1,128]{1,0:T(1,128)} %bitcast.14, f32[1,384]{1,0:T(1,128)} %energy_hbm.1, s32[2]{0:T(128)} %weight_hbm.1), custom_call_target="tpu_custom_call" | custom-call | tf_op jit(solution)/shard_map/pack/pallas_call | solution.py:346
  1.1 29.3 %all_to_all.10 = bf16[64,16,384]{2,1,0:T(8,128)(2,1)S(1)} all-to-all(bf16[64,16,384]{2,1,0:T(8,128)(2,1)S(1)} %get-tuple-element.9), channel_id=1, replica_groups=mesh['freq'=64,'kpt'=2] {'freq'}, dimensions={0} | all-to-all | bytes 1572864 | tf_op jit(solution)/shard_map/all_to_all | solution.py:374
  30.4 16.6 %green.1 = f32[128,128]{1,0:T(8,128)S(1)} custom-call(bf16[1024,384]{1,0:T(8,128)(2,1)S(1)} %bitcast.9, s32[1,128]{1,0:T(1,128)S(1)} %get-tuple-element.10.atom_ref, f32[1,384]{1,0:T(1,128)S(1)} %get-tuple-element.11.energy_ref, f32[1,128]{1,0:T(1,128)S(1)} %get-tuple-element.12.scale_ref), custom_call_target="tpu_custom_call" | custom-call | tf_op jit(solution)/shard_map/green/pallas_call | solution.py:375
  47.0 13.1 %all_to_all.11 = f32[128,1,128]{2,1,0:T(1,128)S(1)} all-to-all(f32[128,1,128]{2,1,0:T(1,128)S(1)} %bitcast.10), channel_id=1, replica_groups=mesh['freq'=64,'kpt'=2] {'freq','kpt'}, dimensions={0} | all-to-all | bytes 131072 | tf_op jit(solution)/shard_map/all_to_all | solution.py:391
  60.1 0.7 %unpack.1 = f32[50,1,64]{2,1,0:T(1,128)} custom-call(f32[128,128]{1,0:T(8,128)S(1)} %bitcast.11), custom_call_target="tpu_custom_call" | custom-call | tf_op jit(solution)/shard_map/unpack/pallas_call | solution.py:394
